TPU v7x, 256 devices: a whole 4x4x8 slice. The times are simulated.
256 devices in a mesh: grp: 64 (over y, x, z_lo, core), blk: 4 (over z_hi).
Axes of the slice: x: 4, y: 4, z: 8 (z_hi: 4, z_lo: 2; z = z_hi * 2 + z_lo), core: 2. Of those that a mesh axis runs over, the one named last changes fastest.
Arguments:
- tokens: bfloat16 [2048, 6144], P(('grp', 'blk')), may hold values from -6 to 6
- norm_gain: bfloat16 [6144], replicated, may hold values from 0.099609375 to 1.8984375
- expert_ids: int32 [2048, 2], P(('grp', 'blk')), may hold values from 0 to 7, all different within a row; in each aligned block of 8 rows (0 to 7, 8 to 15, ...) at most 3 rows name the same one
- combine: float32 [2048, 2], P(('grp', 'blk')), may hold values from 0.2 to 1
- w_gate: bfloat16 [6144, 65536], P(None, ('grp', 'blk')), may hold values from -0.078125 to 0.078125
- w_up: bfloat16 [6144, 65536], P(None, ('grp', 'blk')), may hold values from -0.078125 to 0.078125
- w_down: bfloat16 [65536, 6144], P(('grp', 'blk')), may hold values from -0.0625 to 0.0625
Outputs:
- layer_out: bfloat16 [2048, 6144], P(('grp', 'blk'))
Inputs may be any that keep to these rules, and one draw needn't show every extreme that they name: `expert_ids`: each row names 2 different experts; in the rows of one device no expert is named more than 3 times, a bound that some block reaches.
All inputs are finite; a program needn't handle non-finite values.
Results may differ from a plain program's by a relative error of at most 0.0075.
Values may be sent and summed in bfloat16 or wider, within the bound.
A program may use at most 128 MiB of HBM per device.

v0:
```python
import jax
import jax.numpy as jnp
from jax import lax
from jax.sharding import PartitionSpec as P

E = 8
TOP = 2
CAP = 3


epsilon = 1e-05


def in_order(blocks, dim):
    dims = list(blocks.shape[1:])
    dims[dim] *= blocks.shape[0]
    return jnp.moveaxis(blocks, 0, dim).reshape(dims)


def copy_for_each(x, axis):
    count = lax.axis_size(axis)
    return lax.all_to_all(jnp.broadcast_to(x[None], (count, *x.shape)), axis, 0, 0, tiled=True)


def gathered_copies(x, axis, dim):
    return in_order(copy_for_each(x, axis), dim)


def on_device(tokens, norm_gain, expert_ids, combine, w_gate, w_up, w_down):
    group_count = lax.axis_size("grp")
    per_group = group_count // E
    tok_count = tokens.shape[0]
    model_width = tokens.shape[1]
    wide_tokens = tokens.astype(jnp.float32)
    scale_rows = lax.rsqrt(jnp.mean(wide_tokens * wide_tokens, axis=1, keepdims=True) + epsilon)
    normed = (wide_tokens * scale_rows * norm_gain.astype(jnp.float32)[None, :]).astype(
        jnp.bfloat16
    )
    pair_rows = jnp.repeat(normed, TOP, axis=0)
    route_ids = expert_ids.reshape(tok_count * TOP)
    one_hot = (route_ids[:, None] == jnp.arange(E, dtype=jnp.int32)[None, :]).astype(jnp.int32)
    earlier = jnp.cumsum(one_hot, axis=0) - one_hot
    slot_index = jnp.sum(earlier * one_hot, axis=1)
    slot_match = (
        slot_index[None, None, :] == jnp.arange(CAP, dtype=jnp.int32)[None, :, None]
    ).astype(jnp.int32)
    placer = (one_hot.T[:, None, :] * slot_match).astype(jnp.bfloat16)
    buffer = jnp.einsum(
        "ecp,pd->ecd", placer, pair_rows, preferred_element_type=jnp.float32
    ).astype(jnp.bfloat16)
    stacked = gathered_copies(buffer[None], "blk", 0)
    outgoing = jnp.repeat(stacked, per_group, axis=1)
    arrived = lax.all_to_all(outgoing, "grp", split_axis=1, concat_axis=1, tiled=True)
    shard_rows = arrived.reshape(-1, model_width)
    gate_val = jnp.dot(shard_rows, w_gate, preferred_element_type=jnp.float32)
    up_val = jnp.dot(shard_rows, w_up, preferred_element_type=jnp.float32)
    hidden = (jax.nn.silu(gate_val) * up_val).astype(jnp.bfloat16)
    partial_value = jnp.dot(hidden, w_down, preferred_element_type=jnp.float32)
    rounded = lax.optimization_barrier(partial_value.astype(jnp.bfloat16))
    own_rows = lax.psum_scatter(
        rounded.astype(jnp.float32).astype(jnp.bfloat16), "blk", scatter_dimension=0, tiled=True
    ).astype(jnp.float32)
    home_terms = own_rows.reshape(group_count, CAP, model_width)
    returned = lax.all_to_all(
        home_terms.astype(jnp.bfloat16), "grp", split_axis=0, concat_axis=0, tiled=True
    ).astype(home_terms.dtype)
    expert_out = jnp.sum(returned.reshape(E, per_group, CAP, model_width), axis=1)
    pair_out = expert_out.reshape(E * CAP, model_width)[route_ids * CAP + slot_index]
    expert_mix = jnp.sum(
        pair_out.reshape(tok_count, TOP, model_width) * combine[:, :, None], axis=1
    )
    return (wide_tokens + expert_mix).astype(jnp.bfloat16)


def solution(mesh):
    return jax.shard_map(
        on_device,
        mesh=mesh,
        in_specs=(
            P(("grp", "blk"), None),
            P(),
            P(("grp", "blk"), None),
            P(("grp", "blk"), None),
            P(None, ("grp", "blk")),
            P(None, ("grp", "blk")),
            P(("grp", "blk"), None),
        ),
        out_specs=P(("grp", "blk"), None),
        check_vma=False,
    )
```

profile of v0, /device:TPU:8, one launch (start us, length us, event | category | flops | bytes accessed | tf_op | source)
XLA Modules:
  0.0 485.8 jit_solution(17626698553006937303)
XLA Ops:
  6.5 0.9 copy.16
  7.4 0.1 eq.44
  7.5 0.1 fusion.5
  7.6 0.2 select_reduce_fusion
  7.8 0.7 convert_element_type.55
  8.5 1.1 fusion.1
  9.6 1.0 fusion.3
  10.6 0.1 broadcast_in_dim.6
  10.7 0.1 reshape.134
  10.8 0.2 convolution_convert_fusion.1
  11.0 0.1 broadcast_in_dim.7
  11.1 39.0 %all_to_all.15 = bf16[4,1,8,3,6144]{4,2,3,1,0:T(8,128)(2,1)S(1)} all-to-all(bf16[4,1,8,3,6144]{4,2,3,1,0:T(8,128)(2,1)S(1)} %broadcast_in_dim.7), channel_id=1, replica_groups=mesh['grp'=64,'blk'=4] {'blk'}, dimensions={0} | all-to-all | bytes 2359296 | tf_op jit(solution)/shard_map/all_to_all | solution.py:22
  50.1 0.9 copy.17
  51.1 4.6 broadcast_in_dim.8
  55.7 114.7 %all_to_all.16 = bf16[4,64,3,6144]{3,0,2,1:T(4,128)(2,1)S(1)} all-to-all(bf16[4,64,3,6144]{3,0,2,1:T(4,128)(2,1)S(1)} %bitcast.26), channel_id=1, replica_groups=mesh['grp'=64,'blk'=4] {'grp'}, dimensions={1} | all-to-all | bytes 18874368 | tf_op jit(solution)/shard_map/all_to_all | solution.py:53
  170.4 25.3 %copy.18 = bf16[4,64,3,6144]{3,2,1,0:T(4,128)(2,1)} copy(bf16[4,64,3,6144]{3,0,2,1:T(4,128)(2,1)S(1)} %all_to_all.16) | data formatting | bytes 18874368 | tf_op jit(solution)/shard_map/all_to_all | solution.py:53
  195.7 23.5 %reshape.119 = bf16[768,6144]{1,0:T(8,128)(2,1)} reshape(bf16[4,64,3,6144]{3,2,1,0:T(4,128)(2,1)} %copy.18) | data formatting | bytes 18874368 | tf_op jit(solution)/shard_map/reshape | solution.py:54
  219.2 8.1 %fusion.11 = f32[768,256]{1,0:T(8,128)} fusion(bf16[768,6144]{1,0:T(8,128)(2,1)} %reshape.119, bf16[6144,256]{1,0:T(8,128)(2,1)} %param.11), kind=kOutput, calls=%fused_computation.30 | convolution fusion | flops 2415919104 | bytes 13369344 | tf_op jit(solution)/shard_map/dot_general | solution.py:55
  227.3 19.4 %convolution_convert_fusion = bf16[768,6144]{1,0:T(8,128)(2,1)} fusion(bf16[256,6144]{1,0:T(8,128)(2,1)S(1)} %copy-done, bf16[768,6144]{1,0:T(8,128)(2,1)} %reshape.119, bf16[6144,256]{1,0:T(8,128)(2,1)} %param.12, f32[768,256]{1,0:T(8,128)} %fusion.11), kind=kOutput, calls=%fused_computation.1 | convolution fusion | flops 4837736448 | bytes 25952256 | tf_op jit(solution)/shard_map/dot_general | solution.py:58
  246.7 166.7 %reduce-scatter.2.cloned.1.call-done = bf16[192,6144]{1,0:T(8,128)(2,1)} async-done(((bf16[768,6144]{1,0:T(8,128)(2,1)}), bf16[192,6144]{1,0:T(8,128)(2,1)}) %reduce-scatter.2.cloned.1.call-update) | async-done | bytes 2359312 | tf_op jit(solution)/shard_map/reduce_scatter | solution.py:60
  413.4 6.5 %convert_element_type.60 = bf16[64,3,6144]{2,1,0:T(4,128)(2,1)} reshape(bf16[192,6144]{1,0:T(8,128)(2,1)} %reduce-scatter.2.cloned.1.call-done) | data formatting | bytes 4718592 | tf_op jit(solution)/shard_map/convert_element_type | solution.py:65
  419.9 7.1 %all-to-all-start.2 = ((bf16[64,3,6144]{2,1,0:T(4,128)(2,1)}), bf16[64,3,6144]{2,1,0:T(4,128)(2,1)}, u32[]{:S(2)}, u32[]{:S(2)}) async-start(bf16[64,3,6144]{2,1,0:T(4,128)(2,1)} %convert_element_type.60), calls=%async_computation.3 | async-start | bytes 6291456 | tf_op jit(solution)/shard_map/all_to_all | solution.py:64
  427.0 0.1 copy.19
  427.1 0.1 mul.75
  427.1 0.1 copy.20
  427.2 39.0 %all-to-all-done.2 = bf16[64,3,6144]{2,1,0:T(4,128)(2,1)} async-done(((bf16[64,3,6144]{2,1,0:T(4,128)(2,1)}), bf16[64,3,6144]{2,1,0:T(4,128)(2,1)}, u32[]{:S(2)}, u32[]{:S(2)}) %all-to-all-start.2) | async-done | bytes 2359328 | tf_op jit(solution)/shard_map/all_to_all | solution.py:64
  466.2 4.5 convert_reduce_fusion
  470.8 2.2 reshape.122
  473.0 2.6 gather_fusion
  475.6 1.2 reshape.123
  476.9 0.6 multiply_reduce_fusion
  477.4 1.6 fusion.4
  (15 shorter events, 0.1 us)
Async XLA Ops:
  6.5 220.8 %copy-start = (bf16[256,6144]{1,0:T(8,128)(2,1)S(1)}, bf16[256,6144]{1,0:T(8,128)(2,1)}, u32[]{:S(2)}) copy-start(bf16[256,6144]{1,0:T(8,128)(2,1)} %param.13) | copy-start | bytes 9437188
  6.5 406.9 %reduce-scatter.2.cloned.1.call-start = ((), (), s32[]{:S(2)}) async-start(), calls=%async_computation.4 | async-start | bytes 11796480 | tf_op jit(solution)/shard_map/reduce_scatter | solution.py:60
  419.9 7.1 %copy-start.1 = (s32[8,2]{0,1:T(2,128)S(1)}, s32[8,2]{0,1:T(2,128)}, u32[]{:S(2)}) copy-start(s32[8,2]{0,1:T(2,128)} %param.9) | copy-start | bytes 196
  419.9 7.3 %copy-start.2 = (f32[8,2]{0,1:T(2,128)S(1)}, f32[8,2]{0,1:T(2,128)}, u32[]{:S(2)}) copy-start(f32[8,2]{0,1:T(2,128)} %param.10) | copy-start | bytes 196
  419.9 46.3 %all-to-all-start.2 = ((bf16[64,3,6144]{2,1,0:T(4,128)(2,1)}), bf16[64,3,6144]{2,1,0:T(4,128)(2,1)}, u32[]{:S(2)}, u32[]{:S(2)}) async-start(bf16[64,3,6144]{2,1,0:T(4,128)(2,1)} %convert_element_type.60), calls=%async_computation.3 | async-start | bytes 6291456 | tf_op jit(solution)/shard_map/all_to_all | solution.py:64
Sparse Core Ops, SparseCore 0:
  246.8 166.5 reduce-scatter.1
where the time goes:
time: 490 us; the launch traced here: 486 us
  waiting for transfers between devices  206 us (42%)
  blocking collectives  154 us (31%)
  local copies, waits for them, and re-layouts  68.5 us (14%)
  matrix products  27.6 us (6%)
  between operations  13.5 us (3%)
  other arithmetic  9.71 us (2%)
  starting transfers between devices  7.06 us (1%)
    reduce_scatter x1, waiting for transfers between devices, on_device(): lax.psum_scatter(rounded.astype(jnp.float32).astype(jnp.bfloat16), 'blk',...  167 us
    all_to_all x1, blocking collectives, on_device(): lax.all_to_all(outgoing, 'grp', split_axis=1, concat_axis=1, tiled=True)  115 us
    all_to_all x1, blocking collectives, copy_for_each(): lax.all_to_all(jnp.broadcast_to(x[None], (count, *x.shape)), axis, 0, 0,...  39 us
    all_to_all x1, waiting for transfers between devices, on_device(): lax.all_to_all(home_terms.astype(jnp.bfloat16), 'grp', split_axis=0, conc...  39 us
    all_to_all x1, local copies, waits for them, and re-layouts, on_device(): lax.all_to_all(outgoing, 'grp', split_axis=1, concat_axis=1, tiled=True)  25.3 us
    reshape x1, local copies, waits for them, and re-layouts, on_device(): shard_rows = arrived.reshape(-1, model_width)  23.5 us
    dot_general x1, matrix products, on_device(): partial_value = jnp.dot(hidden, w_down, preferred_element_type=jnp.float32)  19.4 us
  transfers between devices with their start and end apart: 2, of which 2 were waited for; matrix products, arithmetic and copies ran while one was open for 0% of the time, Pallas kernels for 0%

commit v1 on v0

v1 whole, which is shorter than its diff:
```python
import jax
import jax.numpy as jnp
from jax import lax
from jax.experimental import pallas as pl
from jax.experimental.pallas import tpu as pltpu
from jax.sharding import PartitionSpec as P

MESH = pl.DeviceIdType.MESH
D = 6144
HID = 256
QW = D // 4
BLK = 48
EPS = 1e-05
BF = jnp.bfloat16
F32 = jnp.float32


def dot(a, b):
    return jnp.dot(a, b, preferred_element_type=F32)


def iota(shape, dim):
    return lax.broadcasted_iota(jnp.int32, shape, dim)


def kernel(
    tok_ref,
    gain_ref,
    ids_ref,
    comb_ref,
    wg_hbm,
    wu_hbm,
    wd_hbm,
    out_ref,
    wg,
    wu,
    wd,
    sb,
    arr,
    xs,
    ys,
    hid,
    rz,
    rp,
    sums,
    ex,
    home,
    send_sem,
    recv_sem,
    local_sem,
):
    grp = lax.axis_index("grp")
    blk = lax.axis_index("blk")
    core = lax.rem(grp, 2)
    mz = blk * 2 + lax.rem(lax.div(grp, 2), 2)
    mx = lax.rem(lax.div(grp, 4), 4)
    my = lax.div(grp, 16)
    yx = my * 4 + mx
    par = lax.rem(mx, 2)

    def dev(y, x, z, c):
        return (((y * 4 + x) * 2 + lax.rem(z, 2)) * 2 + c, lax.div(z, 2))

    def expert_at(y, x):
        return y * 2 + lax.div(x, 2)

    up = dev(my, mx, lax.rem(mz + 1, 8), core)
    down = dev(my, mx, lax.rem(mz + 7, 8), core)
    pair = dev(my, mx + 1 - 2 * par, mz, core)
    twin = dev(my, mx, mz, 1 - core)
    plane = []
    for d in range(1, 16):
        ty = lax.rem(my + d // 4, 4)
        tx = lax.rem(mx + d % 4, 4)
        plane.append((d, ty, tx))

    barrier = pltpu.get_barrier_semaphore()
    for target in [dev(ty, tx, mz, core) for _, ty, tx in plane] + [up, down, twin]:
        pl.semaphore_signal(barrier, inc=1, device_id=target, device_id_type=MESH)

    local = [
        pltpu.make_async_copy(wg_hbm, wg.at[0], local_sem.at[0]),
        pltpu.make_async_copy(wu_hbm, wu.at[0], local_sem.at[1]),
        pltpu.make_async_copy(wd_hbm, wd.at[pl.ds(0, HID), :], local_sem.at[2]),
    ]
    for copy in local:
        copy.start()

    wide = tok_ref[...].astype(F32)
    scale = lax.rsqrt(jnp.mean(wide * wide, axis=1, keepdims=True) + EPS)
    normed = (wide * scale * gain_ref[...].astype(F32)).astype(BF).astype(F32)
    id0, id1 = ids_ref[:, 0:1], ids_ref[:, 1:2]
    tri = (iota((8, 8), 1) < iota((8, 8), 0)).astype(F32)

    def slots(expert):
        match = ((id0 == expert) | (id1 == expert)).astype(F32)
        return match, dot(tri, match)

    lane = iota((8, 128), 1)
    match, slot = slots(lane >> 4)
    chosen = (match > 0.5) & (slot.astype(jnp.int32) == (lane & 3))
    folded = jnp.zeros((128, QW), F32)
    for q in range(4):
        pick = jnp.where(chosen & (((lane >> 2) & 3) == q), 1.0, 0.0).astype(F32)
        folded += lax.dot_general(
            pick,
            normed[:, q * QW : (q + 1) * QW],
            (((0,), (0,)), ((), ())),
            preferred_element_type=F32,
        )
    sb[...] = folded.astype(BF)
    own_e = pl.multiple_of(expert_at(my, mx) * 16, 16)
    own_j = pl.multiple_of(yx * 16, 16)
    arr[pl.ds(own_j, 16), :] = sb[pl.ds(own_e, 16), :]

    pl.semaphore_wait(barrier, 18)

    sent = []
    counter = [0]

    def remote(src, dst, target, number):
        return pltpu.make_async_remote_copy(
            src_ref=src,
            dst_ref=dst,
            send_sem=send_sem.at[number],
            recv_sem=recv_sem.at[number],
            device_id=target,
            device_id_type=MESH,
        )

    def send(src, dst, target):
        copy = remote(src, dst, target, counter[0])
        counter[0] += 1
        copy.start()
        sent.append(copy)
        return copy

    def rows16(j):
        return pl.ds(pl.multiple_of(j * 16, 16), 16)

    def plane_exchange(source, landing, row_of):
        waits = []
        for d, ty, tx in plane:
            number = counter[0]
            target = dev(ty, tx, mz, core)
            send(source.at[rows16(row_of(ty, tx)), :], landing.at[rows16(yx), :], target)
            fy = lax.rem(my + 4 - d // 4, 4)
            fx = lax.rem(mx + 4 - d % 4, 4)
            waits.append(
                remote(
                    source.at[rows16(row_of(fy, fx)), :],
                    landing.at[rows16(fy * 4 + fx), :],
                    dev(fy, fx, mz, core),
                    number,
                )
            )
        return waits

    scatter = plane_exchange(sb, arr, expert_at)
    weights = [
        send(wg_hbm, wg.at[1], twin),
        send(wu_hbm, wu.at[1], twin),
        send(wd_hbm, wd.at[pl.ds(HID, HID), :], twin),
    ]
    for copy in scatter:
        copy.wait_recv()

    def plane_row(r):
        part = r >> 4
        return (r & 15) + jnp.where(
            part == 0, 0, jnp.where(part == 1, 16 * (1 + par), 16 * (2 - par))
        )

    def fold_mask(row, lane, q):
        c = lane & 3
        return (c < 3) & (((lane >> 2) & 3) == q) & ((lane >> 4) * 3 + c == plane_row(row))

    for q in range(4):
        keep = fold_mask(iota((BLK, 256), 0), iota((BLK, 256), 1), q)
        pick = jnp.where(keep, 1.0, 0.0).astype(BF)
        xs[0:BLK, q * QW : (q + 1) * QW] = dot(pick, arr[...]).astype(BF)

    def part(b, k, count=1):
        return pl.ds(b * BLK + 16 * k, 16 * count)

    def compute(start, rows):
        def gate_up(h, _):
            block = xs[start : start + rows, :]
            gate = dot(block, wg[h])
            upv = dot(block, wu[h])
            value = gate / (1.0 + jnp.exp(-gate)) * upv
            hid[0:rows, pl.ds(pl.multiple_of(h * HID, HID), HID)] = value.astype(BF)
            return 0

        lax.fori_loop(0, 2, gate_up, 0)

        def down_proj(n, _):
            cols = pl.ds(pl.multiple_of(n * 512, 512), 512)
            ys[start : start + rows, cols] = dot(hid[0:rows, :], wd[:, cols]).astype(BF)
            return 0

        lax.fori_loop(0, D // 512, down_proj, 0)

    def z_send(src_b, k, direction, dst_b):
        return send(
            xs.at[part(src_b, k), :], xs.at[part(dst_b, k), :], up if direction else down
        )

    def to_pair(b):
        return send(xs.at[part(b, 1), :], xs.at[part(b, 2), :], pair)

    arriving = {}
    for k in (1, 0):
        arriving[(1, k)] = z_send(0, k, 1, 1)
        arriving[(2, k)] = z_send(0, k, 0, 2)
    theirs = {}
    for copy in local:
        copy.wait()
    for copy in weights:
        copy.wait_recv()
    compute(0, BLK)
    for s in range(1, 5):
        for k in (1, 0):
            for direction in (1, 0):
                b = 2 * s - direction if s < 4 else 7
                if s == 4 and k == direction:
                    continue
                arriving[(b, k)].wait_recv()
                if s < 3:
                    arriving[(b + 2, k)] = z_send(b, k, direction, b + 2)
                elif s == 3 and k != direction:
                    arriving[(7, k)] = z_send(b, k, direction, 7)
                if k == 1:
                    theirs[b] = to_pair(b)
        if s > 1:
            theirs[2 * s - 3].wait_recv()
            theirs[2 * s - 2].wait_recv()
            compute(BLK * (2 * s - 3), 2 * BLK)

    partner_sum = {}

    def give_pair(b):
        partner_sum[b] = send(ys.at[part(b, 2), :], rp.at[pl.ds((b - 1) * 16, 16), :], pair)

    def rz_rows(slot, k):
        return pl.ds(slot * 32 + 16 * k, 16)

    chain = {}

    def pass_on(b, k, direction):
        terms = [ys.at[part(b, k), :]]
        if (b, k) in chain:
            chain[(b, k)].wait_recv()
            terms.append(rz.at[rz_rows(b - 1, k), :])
        if k == 1:
            partner_sum[b].wait_recv()
            terms.append(rp.at[pl.ds((b - 1) * 16, 16), :])
        if len(terms) > 1:
            add_into(ys.at[part(b, k), :], terms)
        if b == 7:
            nxt = 6 if direction else 5
        else:
            nxt = b - 2
        slot = nxt - 1 if nxt > 0 else 6 + direction
        copy = send(
            ys.at[part(b, k), :], rz.at[rz_rows(slot, k), :], up if direction else down
        )
        chain[(nxt if nxt > 0 else ("own", direction), k)] = copy

    def add_into(dst, terms):
        def body(n, _):
            cols = pl.ds(pl.multiple_of(n * 1024, 1024), 1024)
            total = terms[0][:, cols].astype(F32)
            for term in terms[1:]:
                total += term[:, cols].astype(F32)
            dst[:, cols] = total.astype(BF)
            return 0

        lax.fori_loop(0, D // 1024, body, 0)

    give_pair(5)
    give_pair(6)
    pass_on(6, 0, 1)
    theirs[7].wait_recv()
    compute(BLK * 7, BLK)
    give_pair(7)
    pass_on(7, 0, 0)
    for b in (3, 4, 1, 2):
        give_pair(b)
    pass_on(5, 1, 0)
    pass_on(7, 1, 1)
    pass_on(3, 1, 0)
    pass_on(4, 0, 1)
    pass_on(5, 0, 0)
    pass_on(6, 1, 1)
    pass_on(1, 1, 0)
    pass_on(2, 0, 1)
    pass_on(3, 0, 0)
    pass_on(4, 1, 1)
    pass_on(1, 0, 0)
    pass_on(2, 1, 1)
    for k in (0, 1):
        for direction in (0, 1):
            chain[(("own", direction), k)].wait_recv()
        add_into(
            sums.at[pl.ds(16 * k, 16), :],
            [
                ys.at[part(0, k), :],
                rz.at[rz_rows(6, k), :],
                rz.at[rz_rows(7, k), :],
            ],
        )
    sums[32:48, :] = ys[32:48, :]

    expanded = jnp.zeros((256, QW), F32)
    for q in range(4):
        keep = fold_mask(iota((256, BLK), 1), iota((256, BLK), 0), q)
        pick = jnp.where(keep, 1.0, 0.0).astype(BF)
        expanded += dot(pick, sums[:, q * QW : (q + 1) * QW])
    ex[...] = expanded.astype(BF)
    home[pl.ds(own_j, 16), :] = ex[pl.ds(own_j, 16), :]
    back = plane_exchange(ex, home, lambda y, x: y * 4 + x)

    lane = iota((8, 256), 1)
    source = lane >> 4
    expert = (source >> 2) * 2 + ((source & 3) >> 1)
    match, slot = slots(expert)
    weight = jnp.where(id0 == expert, comb_ref[:, 0:1], 0.0) + jnp.where(
        id1 == expert, comb_ref[:, 1:2], 0.0
    )
    chosen = (match > 0.5) & (slot.astype(jnp.int32) == (lane & 3))
    weight = jnp.where(chosen, weight, 0.0)
    high = weight.astype(BF).astype(F32)
    mid = (weight - high).astype(BF).astype(F32)
    low = weight - high - mid
    pieces = jnp.concatenate([high, mid, low], axis=0)
    quarter = (iota((24, 256), 1) >> 2) & 3
    for copy in back:
        copy.wait_recv()
    for q in range(4):
        cols = slice(q * QW, (q + 1) * QW)
        mix = dot(jnp.where(quarter == q, pieces, 0.0).astype(BF), home[...])
        total = mix[0:8] + mix[8:16] + mix[16:24]
        out_ref[:, cols] = (tok_ref[:, cols].astype(F32) + total).astype(BF)
    for copy in sent:
        copy.wait_send()


def on_device(tokens, norm_gain, expert_ids, combine, w_gate, w_up, w_down):
    vmem = pl.BlockSpec(memory_space=pltpu.VMEM)
    hbm = pl.BlockSpec(memory_space=pl.ANY)
    return pl.pallas_call(
        kernel,
        out_shape=jax.ShapeDtypeStruct((8, D), BF),
        in_specs=[vmem] * 4 + [hbm] * 3,
        out_specs=vmem,
        scratch_shapes=[
            pltpu.VMEM((2, D, HID), BF),
            pltpu.VMEM((2, D, HID), BF),
            pltpu.VMEM((2 * HID, D), BF),
            pltpu.VMEM((128, QW), BF),
            pltpu.VMEM((256, QW), BF),
            pltpu.VMEM((8 * BLK, D), BF),
            pltpu.VMEM((8 * BLK, D), BF),
            pltpu.VMEM((2 * BLK, 2 * HID), BF),
            pltpu.VMEM((8 * 32, D), BF),
            pltpu.VMEM((7 * 16, D), BF),
            pltpu.VMEM((BLK, D), BF),
            pltpu.VMEM((256, QW), BF),
            pltpu.VMEM((256, QW), BF),
            pltpu.SemaphoreType.DMA((75,)),
            pltpu.SemaphoreType.DMA((75,)),
            pltpu.SemaphoreType.DMA((3,)),
        ],
        compiler_params=pltpu.CompilerParams(
            collective_id=0, has_side_effects=True, vmem_limit_bytes=60 * 1024 * 1024
        ),
        name="moe",
    )(tokens, norm_gain.reshape(1, D), expert_ids, combine, w_gate, w_up, w_down)


def solution(mesh):
    return jax.shard_map(
        on_device,
        mesh=mesh,
        in_specs=(
            P(("grp", "blk"), None),
            P(),
            P(("grp", "blk"), None),
            P(("grp", "blk"), None),
            P(None, ("grp", "blk")),
            P(None, ("grp", "blk")),
            P(("grp", "blk"), None),
        ),
        out_specs=P(("grp", "blk"), None),
        check_vma=False,
    )
```

time: 490 us -> 124 us (0.25)
  waiting for transfers between devices: 206 us -> 0 us
  blocking collectives: 154 us -> 0 us
  Pallas kernels: 0 us -> 117 us
  local copies, waits for them, and re-layouts: 68.5 us -> 5.56 us
  matrix products: 27.6 us -> 0 us
  between operations: 13.5 us -> 0.01 us
  other arithmetic: 9.71 us -> 0 us
  starting transfers between devices: 7.06 us -> 0 us
    reduce_scatter x1 -> x0, waiting for transfers between devices: 167 us -> none  [on_device(): lax.psum_scatter(rounded.astype(jnp.float32).astype(jnp.bfloat16), 'blk',...]
    all_to_all x2 -> x0, blocking collectives: 154 us -> none  [the longest x1 115 us: on_device(): lax.all_to_all(outgoing, 'grp', split_axis=1, concat_axis=1, tiled=True)]
    pallas_call x0 -> x1, Pallas kernels: none -> 117 us  [on_device(): pl.pallas_call(kernel, out_shape=jax.ShapeDtypeStruct((8, D), BF), in_spe...]
    all_to_all x1 -> x0, waiting for transfers between devices: 39 us -> none  [on_device(): lax.all_to_all(home_terms.astype(jnp.bfloat16), 'grp', split_axis=0, conc...]
    dot_general x3 -> x0, matrix products: 27.6 us -> none  [the longest x1 19.4 us: on_device(): partial_value = jnp.dot(hidden, w_down, preferred_element_type=jnp.float32)]
    reshape x5 -> x1, local copies, waits for them, and re-layouts: 28 us -> 1.33 us  [on_device(): norm_gain.reshape(1, D)]
    all_to_all x1 -> x0, local copies, waits for them, and re-layouts: 25.3 us -> none  [on_device(): lax.all_to_all(outgoing, 'grp', split_axis=1, concat_axis=1, tiled=True)]
    all_to_all x1 -> x0, starting transfers between devices: 7.06 us -> none  [on_device(): lax.all_to_all(home_terms.astype(jnp.bfloat16), 'grp', split_axis=0, conc...]
  transfers between devices with their start and end apart: 2 -> 0, of which waited for: 2 -> 0; matrix products, arithmetic and copies ran while one was open for 0% -> 0% of each run, Pallas kernels for 0% -> 0%
where the time goes in v1:
time: 124 us; the launch traced here: 122 us
  Pallas kernels  117 us (94%)
  local copies, waits for them, and re-layouts  5.56 us (4%)
    pallas_call x1, Pallas kernels, on_device(): pl.pallas_call(kernel, out_shape=jax.ShapeDtypeStruct((8, D), BF), in_spe...  117 us
    unnamed x3, local copies, waits for them, and re-layouts  4.23 us

profile of v1, /device:TPU:8, one launch (start us, length us, event | category | flops | bytes accessed | tf_op | source)
XLA Modules:
  0.0 122.4 jit_solution(8019032645973926152)
XLA Ops:
  0.0 1.3 %copy.8.ids_ref = s32[8,2]{1,0:T(8,128)} copy(s32[8,2]{0,1:T(2,128)} %param.9) | data formatting | bytes 128 | tf_op args[2]
  1.3 1.3 %copy.9.comb_ref = f32[8,2]{1,0:T(8,128)} copy(f32[8,2]{0,1:T(2,128)} %param.10) | data formatting | bytes 128 | tf_op args[3]
  2.7 1.3 %reshape.3.gain_ref = bf16[1,6144]{1,0:T(2,128)(2,1)} reshape(bf16[6144]{0:T(1024)(128)(2,1)} %param.8) | data formatting | bytes 24576 | tf_op jit(solution)/shard_map/reshape | solution.py:379
  4.0 116.9 %moe.1 = bf16[8,6144]{1,0:T(8,128)(2,1)} custom-call(bf16[8,6144]{1,0:T(8,128)(2,1)} %tok_ref.1, bf16[1,6144]{1,0:T(2,128)(2,1)} %reshape.3.gain_ref, s32[8,2]{1,0:T(8,128)} %copy.8.ids_ref, f32[8,2]{1,0:T(8,128)} %copy.9.comb_ref, bf16[6144,256]{1,0:T(8,128)(2,1)} %wg_hbm.1, bf16[6144,256]{1,0:T(8,128)(2,1)} %wu_hbm.1, bf16[256,6144]{1,0:T(8,128)(2,1)} %wd_hbm.1), custom_call_target="tpu_custom_call" | custom-call | tf_op jit(solution)/shard_map/moe/pallas_call | solution.py:352
  120.9 1.5 %copy.11 = bf16[8,6144]{1,0:T(8,128)(2,1)} copy(bf16[8,6144]{1,0:T(8,128)(2,1)} %moe.1) | data formatting | bytes 196608
